TPU v7x, 16 devices: a whole 2x2x2 slice. The times are simulated.
16 devices in a mesh: pp: 2 (over z), dp: 8 (over y, x, core).
Axes of the slice: x: 2, y: 2, z: 2, core: 2. Of those that a mesh axis runs over, the one named last changes fastest.
Arguments:
- tok_ids: int32 [2, 4096], P(None, 'dp')
- d_out: bfloat16 [2, 4096, 128], P('pp', 'dp')
- stored_x: bfloat16 [2, 2, 4096, 128], P('pp', None, 'dp')
- w_in: bfloat16 [24, 128, 512], P('pp')
- w_out: bfloat16 [24, 512, 128], P('pp')
- acc_in: float32 [24, 8, 128, 512], P('pp', 'dp')
- acc_out: float32 [24, 8, 512, 128], P('pp', 'dp')
- acc_emb: float32 [8, 30522, 128], P('dp')
Outputs:
- output 1: float32 [24, 128, 512], P('pp', 'dp')
- output 2: float32 [24, 512, 128], P('pp', 'dp')
- output 3: float32 [30522, 128], P(None, 'dp')
All inputs are finite; a program needn't handle non-finite values.
Results may differ from a plain program's by a relative error of at most 0.0176994.
Values are sent between devices in bfloat16 or wider.
A program may use at most 1 GiB of HBM per device.

v0:
```python
import functools

import jax
import jax.numpy as jnp
from jax import lax
from jax.experimental import pallas as pl
from jax.experimental.pallas import tpu as pltpu
from jax.sharding import PartitionSpec as P

MESH = pl.DeviceIdType.MESH
C0 = 0.7978845608028654
C1 = 0.044715
F32, BF16 = jnp.float32, jnp.bfloat16
ANY = pl.BlockSpec(memory_space=pl.ANY)
VM = pl.BlockSpec(memory_space=pltpu.VMEM)


def coords():
    pp, d = lax.axis_index("pp"), lax.axis_index("dp")
    y, x, c = d // 4, (d // 2) % 2, d % 2
    to_x = {"pp": pp, "dp": d + 2 - 4 * x}
    to_y = {"pp": pp, "dp": d + 4 - 8 * y}
    to_c = {"pp": pp, "dp": d + 1 - 2 * c}
    to_z = {"pp": 1 - pp, "dp": d}
    return pp, y, x, c, to_x, to_y, to_c, to_z


def enter(neighbours):
    barrier = pltpu.get_barrier_semaphore()
    for dev in neighbours:
        pl.semaphore_signal(barrier, inc=1, device_id=dev, device_id_type=MESH)
    pl.semaphore_wait(barrier, len(neighbours))


def remote(src, dst, send, recv, dev):
    return pltpu.make_async_remote_copy(src_ref=src, dst_ref=dst, send_sem=send, recv_sem=recv, device_id=dev, device_id_type=MESH)


def slab_xy(d):
    return (d % 2) * 4 + ((d // 2) % 2) * 2 + d // 4


def slab_yx(d):
    return (d % 2) * 4 + (d // 4) * 2 + (d // 2) % 2


class Reduce:
    def __init__(self, src, r0, r1, r2, sems, to, c, p, q):
        self.src, self.r0, self.r1, self.r2, self.sems, self.to = src, r0, r1, r2, sems, to
        self.c, self.p, self.q = c, p, q

    def copy0(self, i):
        return remote(self.src.at[i, pl.ds(4 * (1 - self.c), 4)], self.r0.at[i], self.sems.at[0, i], self.sems.at[1, i], self.to[0])

    def copy1(self, i):
        at = 4 * self.c + 2 * (1 - self.p)
        return remote(self.src.at[i, pl.ds(at, 2)], self.r1.at[i], self.sems.at[2, i], self.sems.at[3, i], self.to[1])

    def copy2(self, i):
        at = 4 * self.c + 2 * self.p + 1 - self.q
        return remote(self.src.at[i, at], self.r2.at[i], self.sems.at[4, i], self.sems.at[5, i], self.to[2])

    def add0(self, i):
        self.copy0(i).wait_recv()
        for k in range(4):
            at = 4 * self.c + k
            self.src[i, at] = (self.src[i, at].astype(F32) + self.r0[i, k].astype(F32)).astype(BF16)

    def add1(self, i):
        self.copy1(i).wait_recv()
        for k in range(2):
            at = 4 * self.c + 2 * self.p + k
            self.src[i, at] = (self.src[i, at].astype(F32) + self.r1[i, k].astype(F32)).astype(BF16)

    def last(self, i):
        self.copy2(i).wait_recv()
        at = 4 * self.c + 2 * self.p + self.q
        return self.src[i, at].astype(F32) + self.r2[i].astype(F32)

    def drain(self, i):
        self.copy0(i).wait_send()
        self.copy1(i).wait_send()
        self.copy2(i).wait_send()


def dot(a, b, ca, cb):
    return lax.dot_general(a, b, (((ca,), (cb,)), ((), ())), preferred_element_type=F32)


def mlp_kernel(layers, chunks, d_out, x_in, w_in, w_out, acc_in, acc_out, g_in, g_out, dx_out,
               w1, w2, xs, hid, slope, gs, dh, dw1, dw2, acc2, cot_in, dxs,
               s1, s1a, s1b, s1c, s2, s2a, s2b, s2c, wsem, asem, zsem, sem1, sem2):
    pp, y, x, c, to_x, to_y, to_c, to_z = coords()
    tokens = d_out.shape[1]
    rows = tokens // chunks

    def load(i):
        return (pltpu.make_async_copy(w_in.at[i], w1.at[i], wsem.at[0, i]),
                pltpu.make_async_copy(w_out.at[i], w2.at[i], wsem.at[1, i]))

    load_acc1 = pltpu.make_async_copy(acc_in.at[:, 0], dw1, asem.at[0])
    load_acc2 = pltpu.make_async_copy(acc_out.at[:, 0], acc2, asem.at[1])
    for i in range(layers):
        for cp in load(i):
            cp.start()
    load_acc1.start()
    load_acc2.start()
    enter((to_x, to_y, to_c, to_z))

    red1 = Reduce(s1, s1a, s1b, s1c, sem1, (to_c, to_x, to_y), c, x, y)
    red2 = Reduce(s2, s2a, s2b, s2c, sem2, (to_c, to_y, to_x), c, y, x)

    def forward(micro, fresh):
        xs[0] = x_in[0, micro]

        def body(i, carry):
            if fresh:
                for cp in load(i):
                    cp.wait()
            for k in range(chunks):
                r = pl.ds(k * rows, rows)
                xc = xs[i, r]
                h = dot(xc, w1[i], 1, 0).astype(BF16).astype(F32)
                h2 = h * h
                t = jnp.tanh(h * (C0 + (C0 * C1) * h2))
                cdf = 0.5 + 0.5 * t
                a = (h * cdf).astype(BF16)
                hid[i, r] = a
                slope[i, r] = cdf + (0.5 * h) * ((1.0 - t * t) * (C0 + (3.0 * C0 * C1) * h2))
                xs[i + 1, r] = (xc.astype(F32) + dot(a, w2[i], 1, 0)).astype(BF16)
            return carry

        lax.fori_loop(0, layers, body, 0)

    def backward(first, final):
        def block(i):
            for k in range(chunks):
                r = pl.ds(k * rows, rows)
                gc = gs[i + 1, r]
                da = dot(gc, w2[i], 1, 1).astype(BF16).astype(F32)
                dhc = (da * slope[i, r]).astype(BF16)
                dh[r] = dhc
                gs[i, r] = (gc.astype(F32) + dot(dhc, w1[i], 1, 1)).astype(BF16)
            new2 = dot(gs[i + 1], hid[i], 0, 0)
            if not first:
                new2 = new2 + dw2[i]
            new1 = dot(xs[i], dh[...], 0, 0) + dw1[i]
            if not final:
                dw1[i] = new1
                dw2[i] = new2
                return
            new1 = new1.astype(BF16)
            n1 = new1.shape[0] // 8
            for d in range(8):
                s1[i, slab_xy(d)] = new1[d * n1:(d + 1) * n1]
            new2 = (new2.T + acc2[i]).astype(BF16)
            n2 = new2.shape[0] // 8
            for d in range(8):
                s2[i, slab_yx(d)] = new2[d * n2:(d + 1) * n2]

        if not final:
            lax.fori_loop(0, layers, lambda k, carry: (block(layers - 1 - k), carry)[1], 0)
            return

        def stage(k, lag, fn):
            @pl.when((k >= lag) & (k < layers + lag))
            def _():
                fn(layers - 1 - (k - lag))

        def step(k, carry):
            stage(k, 1, lambda i: (red1.copy0(i).start(), red2.copy0(i).start()))
            stage(k, 3, lambda i: (red1.copy1(i).start(), red2.copy1(i).start()))
            stage(k, 6, lambda i: (red1.copy2(i).start(), red2.copy2(i).start()))
            stage(k, 0, block)
            stage(k, 2, lambda i: (red1.add0(i), red2.add0(i)))
            stage(k, 5, lambda i: (red1.add1(i), red2.add1(i)))

            def finish(i):
                g_in[i] = red1.last(i) * 0.125
                g_out[i] = red2.last(i) * 0.125

            stage(k, 8, finish)
            return carry

        lax.fori_loop(0, layers + 9, step, 0)

    send_cot = remote(gs.at[0], cot_in, zsem.at[0], zsem.at[1], to_z)
    send_dx1 = remote(dxs.at[1], dxs.at[1], zsem.at[2], zsem.at[3], to_z)
    send_dx0 = remote(dxs.at[0], dxs.at[0], zsem.at[4], zsem.at[5], to_z)

    @pl.when(pp == 1)
    def _():
        forward(0, True)
        load_acc1.wait()
        load_acc2.wait()
        gs[layers] = d_out[0]
        backward(True, True)
        send_cot.start()
        send_cot.wait_send()
        send_dx1.wait_recv()
        send_dx0.wait_recv()

    @pl.when(pp == 0)
    def _():
        forward(1, True)
        load_acc1.wait()
        load_acc2.wait()
        gs[layers] = d_out[0]
        backward(True, False)
        dxs[1] = gs[0]
        send_dx1.start()
        forward(0, False)
        send_cot.wait_recv()
        gs[layers] = cot_in[...]
        backward(False, True)
        dxs[0] = gs[0]
        send_dx0.start()
        send_dx1.wait_send()
        send_dx0.wait_send()

    dx_out[...] = dxs[...]

    def drain(i, carry):
        red1.drain(i)
        red2.drain(i)
        return carry

    lax.fori_loop(0, layers, drain, 0)


def mlp(d_out, stored_x, w_in, w_out, acc_in, acc_out):
    layers, hid, ff = w_in.shape
    tokens = d_out.shape[1]
    n1, n2 = hid // 8, ff // 8
    return pl.pallas_call(
        functools.partial(mlp_kernel, layers, 4),
        out_shape=(jax.ShapeDtypeStruct((layers, n1, ff), F32), jax.ShapeDtypeStruct((layers, n2, hid), F32),
                   jax.ShapeDtypeStruct((2, tokens, hid), BF16)),
        in_specs=[VM, VM, ANY, ANY, ANY, ANY],
        out_specs=(VM, VM, VM),
        scratch_shapes=[
            pltpu.VMEM((layers, hid, ff), BF16),
            pltpu.VMEM((layers, ff, hid), BF16),
            pltpu.VMEM((layers + 1, tokens, hid), BF16),
            pltpu.VMEM((layers, tokens, ff), BF16),
            pltpu.VMEM((layers, tokens, ff), F32),
            pltpu.VMEM((layers + 1, tokens, hid), BF16),
            pltpu.VMEM((tokens, ff), BF16),
            pltpu.VMEM((layers, hid, ff), F32),
            pltpu.VMEM((layers, hid, ff), F32),
            pltpu.VMEM((layers, ff, hid), F32),
            pltpu.VMEM((tokens, hid), BF16),
            pltpu.VMEM((2, tokens, hid), BF16),
            pltpu.VMEM((layers, 8, n1, ff), BF16),
            pltpu.VMEM((layers, 4, n1, ff), BF16),
            pltpu.VMEM((layers, 2, n1, ff), BF16),
            pltpu.VMEM((layers, n1, ff), BF16),
            pltpu.VMEM((layers, 8, n2, hid), BF16),
            pltpu.VMEM((layers, 4, n2, hid), BF16),
            pltpu.VMEM((layers, 2, n2, hid), BF16),
            pltpu.VMEM((layers, n2, hid), BF16),
            pltpu.SemaphoreType.DMA((2, layers)),
            pltpu.SemaphoreType.DMA((2,)),
            pltpu.SemaphoreType.DMA((6,)),
            pltpu.SemaphoreType.DMA((6, layers)),
            pltpu.SemaphoreType.DMA((6, layers)),
        ],
        compiler_params=pltpu.CompilerParams(collective_id=0, has_side_effects=True, vmem_limit_bytes=63 * 2**20),
    )(d_out, stored_x, w_in, w_out, acc_in, acc_out)


def emb_kernel(pairs, width, rel_ids, dx, acc, out, buf, dxt, sa, sa0, sa1, sa2, sb, sb0, sb1, sb2, fa, fb, za, zb,
               asem, sema, semb, zsem):
    pp, y, x, c, to_x, to_y, to_c, to_z = coords()
    half = 2 * pairs * width
    vocab = acc.shape[0]
    block = 256

    def load(p, size, base):
        return pltpu.make_async_copy(acc.at[pl.ds(base + p * 2 * width, size), 0, :], buf.at[pl.ds(p * 2 * width, size)], asem.at[p])

    def each_load(act):
        for p in range(pairs):
            tail = vocab - half - p * 2 * width
            @pl.when(pp == 0)
            def _():
                act(load(p, 2 * width, 0))

            if tail > 0:
                @pl.when(pp == 1)
                def _():
                    act(load(p, min(2 * width, tail), half))

    each_load(lambda cp: cp.start())
    enter((to_x, to_y, to_c, to_z))
    dxt[...] = dx[...].T
    each_load(lambda cp: cp.wait())

    reda = Reduce(sa, sa0, sa1, sa2, sema, (to_c, to_x, to_y), c, x, y)
    redb = Reduce(sb, sb0, sb1, sb2, semb, (to_c, to_y, to_x), c, y, x)

    def zcopy(i):
        return (remote(fa.at[i], za.at[i], zsem.at[0, i], zsem.at[1, i], to_z),
                remote(fb.at[i], zb.at[i], zsem.at[2, i], zsem.at[3, i], to_z))

    def build(i):
        for part, dst, slab in ((0, sa, slab_xy), (1, sb, slab_yx)):
            def piece(j, carry):
                at = pl.multiple_of(j * block, block)
                row = pl.multiple_of((2 * i + part) * width + j * block, block)
                base = pp * half + row
                ids = rel_ids[...]
                hot = jnp.concatenate([jnp.where(ids == base + 128 * n, 1.0, 0.0).astype(BF16) for n in range(block // 128)], axis=1)
                val = buf[pl.ds(row, block), :].T + dot(dxt[...], hot, 1, 0)
                val = val.astype(BF16)
                for d in range(8):
                    dst[i, slab(d), :, pl.ds(at, block)] = val[d * 16:(d + 1) * 16]
                return carry

            lax.fori_loop(0, width // block, piece, 0)

    def stage(k, lag, fn):
        @pl.when((k >= lag) & (k < pairs + lag))
        def _():
            fn(k - lag)

    def step(k, carry):
        stage(k, 1, lambda i: (reda.copy0(i).start(), redb.copy0(i).start()))
        stage(k, 2, lambda i: (reda.copy1(i).start(), redb.copy1(i).start()))
        stage(k, 4, lambda i: (reda.copy2(i).start(), redb.copy2(i).start()))
        stage(k, 6, lambda i: [cp.start() for cp in zcopy(i)])
        stage(k, 0, build)
        stage(k, 1, lambda i: (reda.add0(i), redb.add0(i)))
        stage(k, 3, lambda i: (reda.add1(i), redb.add1(i)))

        def finish(i):
            fa[i] = reda.last(i).astype(BF16)
            fb[i] = redb.last(i).astype(BF16)

        stage(k, 5, finish)
        return carry

    lax.fori_loop(0, pairs + 7, step, 0)

    def put(i, carry):
        for cp in zcopy(i):
            cp.wait_recv()
        for part, mine, other in ((0, fa, za), (1, fb, zb)):
            off = (2 * i + part) * width
            out[:, pl.ds(pl.multiple_of(pp * half + off, 128), width)] = mine[i]
            out[:, pl.ds(pl.multiple_of((1 - pp) * half + off, 128), width)] = other[i]
        reda.drain(i)
        redb.drain(i)
        for cp in zcopy(i):
            cp.wait_send()
        return carry

    lax.fori_loop(0, pairs, put, 0)


def embed(rel_ids, dx, acc_emb):
    vocab, _, hid = acc_emb.shape
    pairs, width = 6, 1280
    half = 2 * pairs * width
    n = hid // 8
    side = [
        pltpu.VMEM((pairs, 8, n, width), BF16),
        pltpu.VMEM((pairs, 4, n, width), BF16),
        pltpu.VMEM((pairs, 2, n, width), BF16),
        pltpu.VMEM((pairs, n, width), BF16),
    ]
    piece = pltpu.VMEM((pairs, n, width), BF16)
    return pl.pallas_call(
        functools.partial(emb_kernel, pairs, width),
        out_shape=jax.ShapeDtypeStruct((n, 2 * half), BF16),
        in_specs=[VM, VM, ANY],
        out_specs=VM,
        scratch_shapes=[
            pltpu.VMEM((half, hid), F32),
            pltpu.VMEM((hid, dx.shape[0]), BF16),
            *side, *side, piece, piece, piece, piece,
            pltpu.SemaphoreType.DMA((pairs,)),
            pltpu.SemaphoreType.DMA((6, pairs)),
            pltpu.SemaphoreType.DMA((6, pairs)),
            pltpu.SemaphoreType.DMA((4, pairs)),
        ],
        compiler_params=pltpu.CompilerParams(collective_id=1, has_side_effects=True, vmem_limit_bytes=63 * 2**20),
    )(rel_ids, dx, acc_emb)


def solution(mesh):
    def device_body(tok_ids, d_out, stored_x, w_in, w_out, acc_in, acc_out, acc_emb):
        grad_in, grad_out, dx = mlp(d_out, stored_x, w_in, w_out, acc_in, acc_out)
        vocab, hid = acc_emb.shape[1:]
        lane = lax.broadcasted_iota(jnp.int32, (1, 128), 1)
        rel_ids = tok_ids.reshape(-1, 1) - lane
        total = embed(rel_ids, dx.reshape(-1, hid), acc_emb.reshape(vocab, 1, hid))
        grad_emb = total[:, :vocab].T.astype(F32) * 0.125
        return grad_in, grad_out, grad_emb

    return jax.shard_map(
        device_body,
        mesh=mesh,
        in_specs=(P(None, "dp"), P("pp", "dp", None), P("pp", None, "dp", None), P("pp", None, None), P("pp", None, None),
                  P("pp", "dp", None, None), P("pp", "dp", None, None), P("dp", None, None)),
        out_specs=(P("pp", "dp", None), P("pp", "dp", None), P(None, "dp")),
        check_vma=False,
    )
```

profile of v0, /device:TPU:0, one launch (start us, length us, event | category | flops | bytes accessed | tf_op | source)
XLA Modules:
  0.0 130.7 jit_solution(6845049070527894519)
XLA Ops:
  0.6 0.7 copy.11
  1.3 1.0 iota_subtract_fusion.rel_ids
  2.3 87.6 %shard_map.103 = (f32[12,16,512]{2,1,0:T(8,128)}, f32[12,64,128]{2,1,0:T(8,128)}, bf16[2,512,128]{2,1,0:T(8,128)(2,1)}) custom-call(bf16[1,512,128]{2,1,0:T(8,128)(2,1)} %d_out.1, bf16[1,2,512,128]{3,2,1,0:T(8,128)(2,1)} %x_in.1, bf16[12,128,512]{2,1,0:T(8,128)(2,1)} %w_in.1, bf16[12,512,128]{2,1,0:T(8,128)(2,1)} %w_out.1, f32[12,1,128,512]{3,2,1,0:T(8,128)} %acc_in.1, ...), custom_call_target="tpu_custom_call" | custom-call | tf_op jit(solution)/shard_map/pallas_call | solution.py:235
  89.9 36.6 %shard_map.104 = bf16[16,30720]{1,0:T(8,128)(2,1)} custom-call(s32[1024,128]{1,0:T(8,128)} %iota_subtract_fusion.rel_ids, bf16[1024,128]{1,0:T(8,128)(2,1)} %bitcast.7, f32[30522,1,128]{2,1,0:T(1,128)} %bitcast.6), custom_call_target="tpu_custom_call" | custom-call | tf_op jit(solution)/shard_map/pallas_call | solution.py:373
  126.5 0.0 copy-start.1
  126.5 0.0 copy-start
  126.6 2.7 %multiply_bitcast_fusion = f32[30522,16]{0,1:T(8,128)} fusion(bf16[16,30720]{1,0:T(8,128)(2,1)} %shard_map.104), kind=kLoop, calls=%fused_computation | loop fusion | flops 976704 | bytes 2930112 | tf_op jit(solution)/shard_map/mul | solution.py:398
  129.2 0.0 copy-done.1
  129.2 0.7 copy.14
  130.0 0.0 copy-done
  130.0 0.7 copy.15
Async XLA Ops:
  126.5 2.7 %copy-start.1 = (f32[12,16,512]{2,1,0:T(8,128)S(1)}, f32[12,16,512]{2,1,0:T(8,128)}, u32[]{:S(2)}) copy-start(f32[12,16,512]{2,1,0:T(8,128)} %get-tuple-element.12) | copy-start | bytes 1179652
  126.5 3.4 %copy-start = (f32[12,64,128]{2,1,0:T(8,128)S(1)}, f32[12,64,128]{2,1,0:T(8,128)}, u32[]{:S(2)}) copy-start(f32[12,64,128]{2,1,0:T(8,128)} %get-tuple-element.13) | copy-start | bytes 1179652
where the time goes:
time: 131 us
  Pallas kernels  124 us (95%)
  other arithmetic  3.67 us (3%)
  local copies, waits for them, and re-layouts  2.19 us (2%)
    pallas_call x1, Pallas kernels, mlp(): pl.pallas_call(functools.partial(mlp_kernel, layers, 4), out_shape=(jax.S...  87.6 us
    pallas_call x1, Pallas kernels, embed(): pl.pallas_call(functools.partial(emb_kernel, pairs, width), out_shape=jax...  36.6 us
    mul x1, other arithmetic, device_body(): grad_emb = total[:, :vocab].T.astype(F32) * 0.125  2.67 us

commit v1 on v0

--- a/solution.py
+++ b/solution.py
@@ -126,13 +126,13 @@
                 cdf = 0.5 + 0.5 * t
                 a = (h * cdf).astype(BF16)
                 hid[i, r] = a
-                slope[i, r] = cdf + (0.5 * h) * ((1.0 - t * t) * (C0 + (3.0 * C0 * C1) * h2))
+                slope[i, r] = cdf + h * ((cdf * (1.0 - cdf)) * (2.0 * C0 + (6.0 * C0 * C1) * h2))
                 xs[i + 1, r] = (xc.astype(F32) + dot(a, w2[i], 1, 0)).astype(BF16)
             return carry
 
         lax.fori_loop(0, layers, body, 0)
 
-    def backward(first, final):
+    def backward(first, final, send=None):
         def block(i):
             for k in range(chunks):
                 r = pl.ds(k * rows, rows)
@@ -168,6 +168,10 @@
                 fn(layers - 1 - (k - lag))
 
         def step(k, carry):
+            @pl.when(k == layers)
+            def _():
+                send.start()
+
             stage(k, 1, lambda i: (red1.copy0(i).start(), red2.copy0(i).start()))
             stage(k, 3, lambda i: (red1.copy1(i).start(), red2.copy1(i).start()))
             stage(k, 6, lambda i: (red1.copy2(i).start(), red2.copy2(i).start()))
@@ -186,7 +190,7 @@
 
     send_cot = remote(gs.at[0], cot_in, zsem.at[0], zsem.at[1], to_z)
     send_dx1 = remote(dxs.at[1], dxs.at[1], zsem.at[2], zsem.at[3], to_z)
-    send_dx0 = remote(dxs.at[0], dxs.at[0], zsem.at[4], zsem.at[5], to_z)
+    send_dx0 = remote(gs.at[0], dxs.at[0], zsem.at[4], zsem.at[5], to_z)
 
     @pl.when(pp == 1)
     def _():
@@ -194,8 +198,7 @@
         load_acc1.wait()
         load_acc2.wait()
         gs[layers] = d_out[0]
-        backward(True, True)
-        send_cot.start()
+        backward(True, True, send_cot)
         send_cot.wait_send()
         send_dx1.wait_recv()
         send_dx0.wait_recv()
@@ -212,9 +215,8 @@
         forward(0, False)
         send_cot.wait_recv()
         gs[layers] = cot_in[...]
-        backward(False, True)
+        backward(False, True, send_dx0)
         dxs[0] = gs[0]
-        send_dx0.start()
         send_dx1.wait_send()
         send_dx0.wait_send()
 
@@ -233,7 +235,7 @@
     tokens = d_out.shape[1]
     n1, n2 = hid // 8, ff // 8
     return pl.pallas_call(
-        functools.partial(mlp_kernel, layers, 4),
+        functools.partial(mlp_kernel, layers, 1),
         out_shape=(jax.ShapeDtypeStruct((layers, n1, ff), F32), jax.ShapeDtypeStruct((layers, n2, hid), F32),
                    jax.ShapeDtypeStruct((2, tokens, hid), BF16)),
         in_specs=[VM, VM, ANY, ANY, ANY, ANY],

time: 131 us -> 100 us (0.76)
  Pallas kernels: 124 us -> 93.5 us
    pallas_call x1, Pallas kernels: 87.6 us -> 59.4 us  [mlp(): pl.pallas_call(functools.partial(mlp_kernel, layers, 1), out_shape=(jax.S...]
    pallas_call x1, Pallas kernels: 36.6 us -> 34.1 us  [embed(): pl.pallas_call(functools.partial(emb_kernel, pairs, width), out_shape=jax...]
where the time goes in v1:
time: 100 us
  Pallas kernels  93.5 us (94%)
  other arithmetic  3.67 us (4%)
  local copies, waits for them, and re-layouts  2.19 us (2%)
    pallas_call x1, Pallas kernels, mlp(): pl.pallas_call(functools.partial(mlp_kernel, layers, 1), out_shape=(jax.S...  59.4 us
    pallas_call x1, Pallas kernels, embed(): pl.pallas_call(functools.partial(emb_kernel, pairs, width), out_shape=jax...  34.1 us
    mul x1, other arithmetic, device_body(): grad_emb = total[:, :vocab].T.astype(F32) * 0.125  2.67 us
    unnamed x7, local copies, waits for them, and re-layouts  2.19 us

profile of v1, /device:TPU:0, one launch (start us, length us, event | category | flops | bytes accessed | tf_op | source)
XLA Modules:
  0.0 100.1 jit_solution(13903162613938253127)
XLA Ops:
  0.6 0.7 copy.11
  1.3 1.0 iota_subtract_fusion.rel_ids
  2.3 59.4 %shard_map.103 = (f32[12,16,512]{2,1,0:T(8,128)}, f32[12,64,128]{2,1,0:T(8,128)}, bf16[2,512,128]{2,1,0:T(8,128)(2,1)}) custom-call(bf16[1,512,128]{2,1,0:T(8,128)(2,1)} %d_out.1, bf16[1,2,512,128]{3,2,1,0:T(8,128)(2,1)} %x_in.1, bf16[12,128,512]{2,1,0:T(8,128)(2,1)} %w_in.1, bf16[12,512,128]{2,1,0:T(8,128)(2,1)} %w_out.1, f32[12,1,128,512]{3,2,1,0:T(8,128)} %acc_in.1, ...), custom_call_target="tpu_custom_call" | custom-call | tf_op jit(solution)/shard_map/pallas_call | solution.py:237
  61.8 34.1 %shard_map.104 = bf16[16,30720]{1,0:T(8,128)(2,1)} custom-call(s32[1024,128]{1,0:T(8,128)} %iota_subtract_fusion.rel_ids, bf16[1024,128]{1,0:T(8,128)(2,1)} %bitcast.7, f32[30522,1,128]{2,1,0:T(1,128)} %bitcast.6), custom_call_target="tpu_custom_call" | custom-call | tf_op jit(solution)/shard_map/pallas_call | solution.py:375
  95.9 0.0 copy-start.1
  95.9 0.0 copy-start
  95.9 2.7 %multiply_bitcast_fusion = f32[30522,16]{0,1:T(8,128)} fusion(bf16[16,30720]{1,0:T(8,128)(2,1)} %shard_map.104), kind=kLoop, calls=%fused_computation | loop fusion | flops 976704 | bytes 2930112 | tf_op jit(solution)/shard_map/mul | solution.py:400
  98.6 0.0 copy-done.1
  98.6 0.7 copy.14
  99.3 0.0 copy-done
  99.3 0.7 copy.15
Async XLA Ops:
  95.9 2.7 %copy-start.1 = (f32[12,16,512]{2,1,0:T(8,128)S(1)}, f32[12,16,512]{2,1,0:T(8,128)}, u32[]{:S(2)}) copy-start(f32[12,16,512]{2,1,0:T(8,128)} %get-tuple-element.12) | copy-start | bytes 1179652
  95.9 3.4 %copy-start = (f32[12,64,128]{2,1,0:T(8,128)S(1)}, f32[12,64,128]{2,1,0:T(8,128)}, u32[]{:S(2)}) copy-start(f32[12,64,128]{2,1,0:T(8,128)} %get-tuple-element.13) | copy-start | bytes 1179652

commit v2 on v1

v2 whole, which is shorter than its diff:
```python
import functools

import jax
import jax.numpy as jnp
from jax import lax
from jax.experimental import pallas as pl
from jax.experimental.pallas import tpu as pltpu
from jax.sharding import PartitionSpec as P

MESH = pl.DeviceIdType.MESH
C0 = 0.7978845608028654
C1 = 0.044715
F32, BF16 = jnp.float32, jnp.bfloat16
ANY = pl.BlockSpec(memory_space=pl.ANY)
VM = pl.BlockSpec(memory_space=pltpu.VMEM)


def coords():
    pp, d = lax.axis_index("pp"), lax.axis_index("dp")
    y, x, c = d // 4, (d // 2) % 2, d % 2
    to_x = {"pp": pp, "dp": d + 2 - 4 * x}
    to_y = {"pp": pp, "dp": d + 4 - 8 * y}
    to_c = {"pp": pp, "dp": d + 1 - 2 * c}
    to_z = {"pp": 1 - pp, "dp": d}
    return pp, y, x, c, to_x, to_y, to_c, to_z


def enter(neighbours):
    barrier = pltpu.get_barrier_semaphore()
    for dev in neighbours:
        pl.semaphore_signal(barrier, inc=1, device_id=dev, device_id_type=MESH)
    pl.semaphore_wait(barrier, len(neighbours))


def remote(src, dst, send, recv, dev):
    return pltpu.make_async_remote_copy(src_ref=src, dst_ref=dst, send_sem=send, recv_sem=recv, device_id=dev, device_id_type=MESH)


def slab_xy(d):
    return (d % 2) * 4 + ((d // 2) % 2) * 2 + d // 4


def slab_yx(d):
    return (d % 2) * 4 + (d // 4) * 2 + (d // 2) % 2


class Reduce:
    def __init__(self, src, r0, r1, r2, sems, to, c, p, q):
        self.src, self.r0, self.r1, self.r2, self.sems, self.to = src, r0, r1, r2, sems, to
        self.c, self.p, self.q = c, p, q

    def copy0(self, i):
        return remote(self.src.at[i, pl.ds(4 * (1 - self.c), 4)], self.r0.at[i], self.sems.at[0, i], self.sems.at[1, i], self.to[0])

    def copy1(self, i):
        at = 4 * self.c + 2 * (1 - self.p)
        return remote(self.src.at[i, pl.ds(at, 2)], self.r1.at[i], self.sems.at[2, i], self.sems.at[3, i], self.to[1])

    def copy2(self, i):
        at = 4 * self.c + 2 * self.p + 1 - self.q
        return remote(self.src.at[i, at], self.r2.at[i], self.sems.at[4, i], self.sems.at[5, i], self.to[2])

    def add0(self, i):
        self.copy0(i).wait_recv()
        for k in range(4):
            at = 4 * self.c + k
            self.src[i, at] = (self.src[i, at].astype(F32) + self.r0[i, k].astype(F32)).astype(BF16)

    def add1(self, i):
        self.copy1(i).wait_recv()
        for k in range(2):
            at = 4 * self.c + 2 * self.p + k
            self.src[i, at] = (self.src[i, at].astype(F32) + self.r1[i, k].astype(F32)).astype(BF16)

    def last(self, i):
        self.copy2(i).wait_recv()
        at = 4 * self.c + 2 * self.p + self.q
        return self.src[i, at].astype(F32) + self.r2[i].astype(F32)

    def drain(self, i):
        self.copy0(i).wait_send()
        self.copy1(i).wait_send()
        self.copy2(i).wait_send()


def dot(a, b, ca, cb):
    return lax.dot_general(a, b, (((ca,), (cb,)), ((), ())), preferred_element_type=F32)


def fused_kernel(layers, pairs, width, vocab, tok_ids, d_out, x_in, w_in, w_out, acc_in, acc_out, acc_emb, g_in, g_out, emb_out,
                 w1, w2, xs, hid, slope, gs, dh, dw1, dw2, acc2, cot_in, dxs, s1, s1a, s1b, s1c, s2, s2a, s2b, s2c,
                 rel, buf, dxt, sa, sa0, sa1, sa2, sb, sb0, sb1, sb2, fa, fb, za, zb,
                 wsem, asem, zsem, sem1, sem2, esem, sema, semb, fsem):
    pp, y, x, c, to_x, to_y, to_c, to_z = coords()
    tokens = dxs.shape[1]
    half = 2 * pairs * width
    block = 256

    def load(i):
        return (pltpu.make_async_copy(w_in.at[i], w1.at[i], wsem.at[0, i]),
                pltpu.make_async_copy(w_out.at[i], w2.at[i], wsem.at[1, i]))

    def load_emb(act):
        def one(size, base):
            act(pltpu.make_async_copy(acc_emb.at[pl.ds(base, size), 0, :], buf.at[pl.ds(0, size)], esem))

        @pl.when(pp == 0)
        def _():
            one(half, 0)

        @pl.when(pp == 1)
        def _():
            one(vocab - half, half)

    load_x = pltpu.make_async_copy(x_in.at[0, 1 - pp], xs.at[0], asem.at[2])
    load_g = pltpu.make_async_copy(d_out.at[0], gs.at[layers], asem.at[3])
    load_x.start()
    load_g.start()
    load_acc1 = pltpu.make_async_copy(acc_in.at[:, 0], dw1, asem.at[0])
    load_acc2 = pltpu.make_async_copy(acc_out.at[:, 0], acc2, asem.at[1])
    for i in range(layers):
        for cp in load(i):
            cp.start()
    load_acc1.start()
    load_acc2.start()
    load_emb(lambda cp: cp.start())
    enter((to_x, to_y, to_c, to_z))

    lane = lax.broadcasted_iota(jnp.int32, (128, 128), 1)
    for j in range(2):
        for b in range(tokens // 128):
            ids = tok_ids[j:j + 1, b * 128:(b + 1) * 128].astype(F32)
            ids = jnp.broadcast_to(ids, (128, 128)).T.astype(jnp.int32)
            rel[pl.ds(j * tokens + b * 128, 128)] = ids - lane
    load_x.wait()

    red1 = Reduce(s1, s1a, s1b, s1c, sem1, (to_c, to_x, to_y), c, x, y)
    red2 = Reduce(s2, s2a, s2b, s2c, sem2, (to_c, to_y, to_x), c, y, x)
    reda = Reduce(sa, sa0, sa1, sa2, sema, (to_c, to_x, to_y), c, x, y)
    redb = Reduce(sb, sb0, sb1, sb2, semb, (to_c, to_y, to_x), c, y, x)

    def forward(fresh):
        def body(i, carry):
            if fresh:
                for cp in load(i):
                    cp.wait()
            xc = xs[i]
            h = dot(xc, w1[i], 1, 0).astype(BF16).astype(F32)
            h2 = h * h
            t = jnp.tanh(h * (C0 + (C0 * C1) * h2))
            cdf = 0.5 + 0.5 * t
            a = (h * cdf).astype(BF16)
            hid[i] = a
            slope[i] = cdf + h * ((cdf * (1.0 - cdf)) * (2.0 * C0 + (6.0 * C0 * C1) * h2))
            xs[i + 1] = (xc.astype(F32) + dot(a, w2[i], 1, 0)).astype(BF16)
            return carry

        lax.fori_loop(0, layers, body, 0)

    def block_backward(i, first, final):
        gc = gs[i + 1]
        da = dot(gc, w2[i], 1, 1).astype(BF16).astype(F32)
        dhc = (da * slope[i]).astype(BF16)
        dh[...] = dhc
        gs[i] = (gc.astype(F32) + dot(dhc, w1[i], 1, 1)).astype(BF16)
        new2 = dot(gs[i + 1], hid[i], 0, 0)
        if not first:
            new2 = new2 + dw2[i]
        new1 = dot(xs[i], dh[...], 0, 0) + dw1[i]
        if not final:
            dw1[i] = new1
            dw2[i] = new2
            return
        new1 = new1.astype(BF16)
        n1 = new1.shape[0] // 8
        for d in range(8):
            s1[i, slab_xy(d)] = new1[d * n1:(d + 1) * n1]
        new2 = (new2.T + acc2[i]).astype(BF16)
        n2 = new2.shape[0] // 8
        for d in range(8):
            s2[i, slab_yx(d)] = new2[d * n2:(d + 1) * n2]

    def start0(i):
        red1.copy0(i).start()
        red2.copy0(i).start()

    def start1(i):
        red1.copy1(i).start()
        red2.copy1(i).start()

    def start2(i):
        red1.copy2(i).start()
        red2.copy2(i).start()

    def add0(i):
        red1.add0(i)
        red2.add0(i)

    def add1(i):
        red1.add1(i)
        red2.add1(i)

    def finish(i):
        g_in[i] = red1.last(i)
        g_out[i] = red2.last(i)

    def when_layer(k, lag, fn):
        @pl.when((k >= lag) & (k < layers + lag))
        def _():
            fn(layers - 1 - (k - lag))

    send_cot = remote(gs.at[0], cot_in, zsem.at[0], zsem.at[1], to_z)
    send_dx1 = remote(dxs.at[1], dxs.at[1], zsem.at[2], zsem.at[3], to_z)
    send_dx0 = remote(gs.at[0], dxs.at[0], zsem.at[4], zsem.at[5], to_z)

    @pl.when(pp == 1)
    def _():
        forward(True)
        load_acc1.wait()
        load_acc2.wait()
        load_g.wait()

        def step(k, carry):
            @pl.when(k == layers)
            def _():
                send_cot.start()

            when_layer(k, 1, start0)
            when_layer(k, 3, start1)
            when_layer(k, 6, start2)
            when_layer(k, 0, lambda i: block_backward(i, True, True))
            when_layer(k, 2, add0)
            when_layer(k, 5, add1)
            when_layer(k, 8, finish)
            return carry

        lax.fori_loop(0, layers + 9, step, 0)
        send_cot.wait_send()
        send_dx1.wait_recv()
        dxt[:, pl.ds(tokens, tokens)] = dxs[1].T
        send_dx0.wait_recv()
        dxt[:, pl.ds(0, tokens)] = dxs[0].T

    @pl.when(pp == 0)
    def _():
        next_x = pltpu.make_async_copy(x_in.at[0, 0], dxs.at[0], asem.at[4])
        next_x.start()
        forward(True)
        load_acc1.wait()
        load_acc2.wait()
        load_g.wait()

        def back(k, carry):
            block_backward(layers - 1 - k, True, False)
            return carry

        lax.fori_loop(0, layers, back, 0)
        dxs[1] = gs[0]
        send_dx1.start()
        next_x.wait()
        xs[0] = dxs[0]
        forward(False)
        dxt[:, pl.ds(tokens, tokens)] = dxs[1].T
        send_cot.wait_recv()
        gs[layers] = cot_in[...]

        def step(k, carry):
            @pl.when(k == layers)
            def _():
                send_dx0.start()

            when_layer(k, 1, start0)
            when_layer(k, 3, start1)
            when_layer(k, 0, lambda i: block_backward(i, False, True))
            when_layer(k, 2, add0)
            return carry

        lax.fori_loop(0, layers + 4, step, 0)
        dxt[:, pl.ds(0, tokens)] = gs[0].T
        send_dx1.wait_send()
        send_dx0.wait_send()

    load_emb(lambda cp: cp.wait())

    def zcopy(i):
        return (remote(fa.at[i], za.at[i], fsem.at[0, i], fsem.at[1, i], to_z),
                remote(fb.at[i], zb.at[i], fsem.at[2, i], fsem.at[3, i], to_z))

    def build(i):
        for part, dst, slab in ((0, sa, slab_xy), (1, sb, slab_yx)):
            def piece(j, carry):
                at = pl.multiple_of(j * block, block)
                row = pl.multiple_of((2 * i + part) * width + j * block, block)
                base = pp * half + row
                ids = rel[...]
                hot = jnp.concatenate([jnp.where(ids == base + 128 * n, 1.0, 0.0).astype(BF16) for n in range(block // 128)], axis=1)
                val = buf[pl.ds(row, block), :].T + dot(dxt[...], hot, 1, 0)
                val = val.astype(BF16)
                for d in range(8):
                    dst[i, slab(d), :, pl.ds(at, block)] = val[d * 16:(d + 1) * 16]
                return carry

            lax.fori_loop(0, width // block, piece, 0)

    def emb_finish(i):
        fa[i] = reda.last(i).astype(BF16)
        fb[i] = redb.last(i).astype(BF16)

    def put(i):
        for cp in zcopy(i):
            cp.wait_recv()
        for part, mine, other in ((0, fa, za), (1, fb, zb)):
            off = (2 * i + part) * width
            emb_out[:, pl.ds(pl.multiple_of(pp * half + off, 128), width)] = mine[i]
            emb_out[:, pl.ds(pl.multiple_of((1 - pp) * half + off, 128), width)] = other[i]

    def emb_step(k, carry):
        def stage(lag, fn):
            @pl.when((k >= lag) & (k < pairs + lag))
            def _():
                fn(k - lag)

        def late(lag, fn):
            for n in range(2):
                at = 2 * (k - lag) + n

                @pl.when((pp == 0) & (at >= 0) & (at < layers))
                def _():
                    fn(layers - 1 - at)

        late(1, start2)
        stage(1, lambda i: (reda.copy0(i).start(), redb.copy0(i).start()))
        stage(2, lambda i: (reda.copy1(i).start(), redb.copy1(i).start()))
        stage(4, lambda i: (reda.copy2(i).start(), redb.copy2(i).start()))
        stage(6, lambda i: [cp.start() for cp in zcopy(i)])
        stage(0, build)
        late(0, add1)
        stage(1, lambda i: (reda.add0(i), redb.add0(i)))
        stage(3, lambda i: (reda.add1(i), redb.add1(i)))
        stage(5, emb_finish)
        late(4, finish)
        stage(8, put)
        return carry

    lax.fori_loop(0, pairs + 9, emb_step, 0)

    def drain_layer(i, carry):
        red1.drain(i)
        red2.drain(i)
        return carry

    lax.fori_loop(0, layers, drain_layer, 0)

    def drain_pair(i, carry):
        reda.drain(i)
        redb.drain(i)
        for cp in zcopy(i):
            cp.wait_send()
        return carry

    lax.fori_loop(0, pairs, drain_pair, 0)


def fused(tok_ids, d_out, stored_x, w_in, w_out, acc_in, acc_out, acc_emb):
    layers, hid, ff = w_in.shape
    tokens = d_out.shape[1]
    vocab = acc_emb.shape[0]
    pairs, width = 10, 768
    half = 2 * pairs * width
    n1, n2 = hid // 8, ff // 8

    def side(count, *shape):
        return [pltpu.VMEM((count, 8, *shape), BF16), pltpu.VMEM((count, 4, *shape), BF16),
                pltpu.VMEM((count, 2, *shape), BF16), pltpu.VMEM((count, *shape), BF16)]

    piece = pltpu.VMEM((pairs, n1, width), BF16)
    return pl.pallas_call(
        functools.partial(fused_kernel, layers, pairs, width, vocab),
        out_shape=(jax.ShapeDtypeStruct((layers, n1, ff), F32), jax.ShapeDtypeStruct((layers, n2, hid), F32),
                   jax.ShapeDtypeStruct((n1, 2 * half), BF16)),
        in_specs=[VM, ANY, ANY, ANY, ANY, ANY, ANY, ANY],
        out_specs=(VM, VM, VM),
        scratch_shapes=[
            pltpu.VMEM((layers, hid, ff), BF16),
            pltpu.VMEM((layers, ff, hid), BF16),
            pltpu.VMEM((layers + 1, tokens, hid), BF16),
            pltpu.VMEM((layers, tokens, ff), BF16),
            pltpu.VMEM((layers, tokens, ff), F32),
            pltpu.VMEM((layers + 1, tokens, hid), BF16),
            pltpu.VMEM((tokens, ff), BF16),
            pltpu.VMEM((layers, hid, ff), F32),
            pltpu.VMEM((layers, hid, ff), F32),
            pltpu.VMEM((layers, ff, hid), F32),
            pltpu.VMEM((tokens, hid), BF16),
            pltpu.VMEM((2, tokens, hid), BF16),
            *side(layers, n1, ff),
            *side(layers, n2, hid),
            pltpu.VMEM((2 * tokens, 128), jnp.int32),
            pltpu.VMEM((half, hid), F32),
            pltpu.VMEM((hid, 2 * tokens), BF16),
            *side(pairs, n1, width),
            *side(pairs, n1, width),
            piece, piece, piece, piece,
            pltpu.SemaphoreType.DMA((2, layers)),
            pltpu.SemaphoreType.DMA((5,)),
            pltpu.SemaphoreType.DMA((6,)),
            pltpu.SemaphoreType.DMA((6, layers)),
            pltpu.SemaphoreType.DMA((6, layers)),
            pltpu.SemaphoreType.DMA,
            pltpu.SemaphoreType.DMA((6, pairs)),
            pltpu.SemaphoreType.DMA((6, pairs)),
            pltpu.SemaphoreType.DMA((4, pairs)),
        ],
        compiler_params=pltpu.CompilerParams(collective_id=0, has_side_effects=True, vmem_limit_bytes=67043328),
    )(tok_ids, d_out, stored_x, w_in, w_out, acc_in, acc_out, acc_emb)


def mean_kernel(a, b, e, g_in, g_out, g_emb):
    g_in[...] = a[...] * 0.125
    g_out[...] = b[...] * 0.125
    g_emb[...] = e[:, :g_emb.shape[1]].astype(F32) * 0.125


def mean(a, b, e, vocab):
    return pl.pallas_call(
        mean_kernel,
        out_shape=(jax.ShapeDtypeStruct(a.shape, F32), jax.ShapeDtypeStruct(b.shape, F32), jax.ShapeDtypeStruct((e.shape[0], vocab), F32)),
        in_specs=[VM, VM, VM],
        out_specs=(VM, VM, VM),
    )(a, b, e)


def solution(mesh):
    def device_body(tok_ids, d_out, stored_x, w_in, w_out, acc_in, acc_out, acc_emb):
        vocab, hid = acc_emb.shape[1:]
        sums = fused(tok_ids, d_out, stored_x, w_in, w_out, acc_in, acc_out, acc_emb.reshape(vocab, 1, hid))
        grad_in, grad_out, grad_emb = mean(*sums, vocab)
        return grad_in, grad_out, grad_emb.T

    return jax.shard_map(
        device_body,
        mesh=mesh,
        in_specs=(P(None, "dp"), P("pp", "dp", None), P("pp", None, "dp", None), P("pp", None, None), P("pp", None, None),
                  P("pp", "dp", None, None), P("pp", "dp", None, None), P("dp", None, None)),
        out_specs=(P("pp", "dp", None), P("pp", "dp", None), P(None, "dp")),
        check_vma=False,
    )
```

time: 100 us -> 87.9 us (0.88)
  Pallas kernels: 93.5 us -> 87.1 us
  other arithmetic: 3.67 us -> 0 us
  local copies, waits for them, and re-layouts: 2.19 us -> 0 us
    pallas_call x2, Pallas kernels: 93.5 us -> 87.1 us  [the longest x1 84.1 us: fused(): pl.pallas_call(functools.partial(fused_kernel, layers, pairs, width, voca...]
    mul x1 -> x0, other arithmetic: 2.67 us -> none  [device_body(): grad_emb = total[:, :vocab].T.astype(F32) * 0.125]
    unnamed x7 -> x0, local copies, waits for them, and re-layouts: 2.19 us -> none
where the time goes in v2:
time: 87.9 us; the launch traced here: 87.7 us
  Pallas kernels  87.1 us (99%)
    pallas_call x1, Pallas kernels, fused(): pl.pallas_call(functools.partial(fused_kernel, layers, pairs, width, voca...  84.1 us
    pallas_call x1, Pallas kernels, mean(): pl.pallas_call(mean_kernel, out_shape=(jax.ShapeDtypeStruct(a.shape, F32)...  3.03 us

profile of v2, /device:TPU:0, one launch (start us, length us, event | category | flops | bytes accessed | tf_op | source)
XLA Modules:
  0.0 87.7 jit_solution(5330388631498683124)
XLA Ops:
  0.6 84.1 %shard_map.103 = (f32[12,16,512]{2,1,0:T(8,128)}, f32[12,64,128]{2,1,0:T(8,128)}, bf16[16,30720]{1,0:T(8,128)(2,1)}) custom-call(s32[2,512]{1,0:T(2,128)} %tok_ids.1, bf16[1,512,128]{2,1,0:T(8,128)(2,1)} %d_out.1, bf16[1,2,512,128]{3,2,1,0:T(8,128)(2,1)} %x_in.1, bf16[12,128,512]{2,1,0:T(8,128)(2,1)} %w_in.1, bf16[12,512,128]{2,1,0:T(8,128)(2,1)} %w_out.1, ...), custom_call_target="tpu_custom_call" | custom-call | tf_op jit(solution)/shard_map/pallas_call | solution.py:377
  84.7 3.0 %shard_map.104 = (f32[12,16,512]{2,1,0:T(8,128)}, f32[12,64,128]{2,1,0:T(8,128)}, f32[16,30522]{1,0:T(8,128)}) custom-call(f32[12,16,512]{2,1,0:T(8,128)} %get-tuple-element.9.a, f32[12,64,128]{2,1,0:T(8,128)} %get-tuple-element.10.b, bf16[16,30720]{1,0:T(8,128)(2,1)} %get-tuple-element.11.e), custom_call_target="tpu_custom_call" | custom-call | tf_op jit(solution)/shard_map/pallas_call | solution.py:425

commit v3 on v2

--- a/solution.py
+++ b/solution.py
@@ -94,7 +94,7 @@
     pp, y, x, c, to_x, to_y, to_c, to_z = coords()
     tokens = dxs.shape[1]
     half = 2 * pairs * width
-    block = 256
+    block = width
 
     def load(i):
         return (pltpu.make_async_copy(w_in.at[i], w1.at[i], wsem.at[0, i]),

time: 87.9 us -> 87.1 us (level)
  no operation moved by 1% of the time
where the time goes in v3:
time: 87.1 us; the launch traced here: 87 us
  Pallas kernels  86.3 us (99%)
    pallas_call x1, Pallas kernels, fused(): pl.pallas_call(functools.partial(fused_kernel, layers, pairs, width, voca...  83.3 us
    pallas_call x1, Pallas kernels, mean(): pl.pallas_call(mean_kernel, out_shape=(jax.ShapeDtypeStruct(a.shape, F32)...  3.03 us

profile of v3, /device:TPU:0, one launch (start us, length us, event | category | flops | bytes accessed | tf_op | source)
XLA Modules:
  0.0 87.0 jit_solution(2721465083748378041)
XLA Ops:
  0.6 83.3 %shard_map.103 = (f32[12,16,512]{2,1,0:T(8,128)}, f32[12,64,128]{2,1,0:T(8,128)}, bf16[16,30720]{1,0:T(8,128)(2,1)}) custom-call(s32[2,512]{1,0:T(2,128)} %tok_ids.1, bf16[1,512,128]{2,1,0:T(8,128)(2,1)} %d_out.1, bf16[1,2,512,128]{3,2,1,0:T(8,128)(2,1)} %x_in.1, bf16[12,128,512]{2,1,0:T(8,128)(2,1)} %w_in.1, bf16[12,512,128]{2,1,0:T(8,128)(2,1)} %w_out.1, ...), custom_call_target="tpu_custom_call" | custom-call | tf_op jit(solution)/shard_map/pallas_call | solution.py:377
  84.0 3.0 %shard_map.104 = (f32[12,16,512]{2,1,0:T(8,128)}, f32[12,64,128]{2,1,0:T(8,128)}, f32[16,30522]{1,0:T(8,128)}) custom-call(f32[12,16,512]{2,1,0:T(8,128)} %get-tuple-element.9.a, f32[12,64,128]{2,1,0:T(8,128)} %get-tuple-element.10.b, bf16[16,30720]{1,0:T(8,128)(2,1)} %get-tuple-element.11.e), custom_call_target="tpu_custom_call" | custom-call | tf_op jit(solution)/shard_map/pallas_call | solution.py:425

commit v4 on v3

--- a/solution.py
+++ b/solution.py
@@ -25,11 +25,11 @@
     return pp, y, x, c, to_x, to_y, to_c, to_z
 
 
-def enter(neighbours):
+def knock(neighbours):
     barrier = pltpu.get_barrier_semaphore()
     for dev in neighbours:
         pl.semaphore_signal(barrier, inc=1, device_id=dev, device_id_type=MESH)
-    pl.semaphore_wait(barrier, len(neighbours))
+    return lambda: pl.semaphore_wait(barrier, len(neighbours))
 
 
 def remote(src, dst, send, recv, dev):
@@ -114,17 +114,13 @@
 
     load_x = pltpu.make_async_copy(x_in.at[0, 1 - pp], xs.at[0], asem.at[2])
     load_g = pltpu.make_async_copy(d_out.at[0], gs.at[layers], asem.at[3])
-    load_x.start()
-    load_g.start()
     load_acc1 = pltpu.make_async_copy(acc_in.at[:, 0], dw1, asem.at[0])
     load_acc2 = pltpu.make_async_copy(acc_out.at[:, 0], acc2, asem.at[1])
+    enter = knock((to_x, to_y, to_c, to_z))
+    load_x.start()
     for i in range(layers):
         for cp in load(i):
             cp.start()
-    load_acc1.start()
-    load_acc2.start()
-    load_emb(lambda cp: cp.start())
-    enter((to_x, to_y, to_c, to_z))
 
     lane = lax.broadcasted_iota(jnp.int32, (128, 128), 1)
     for j in range(2):
@@ -139,11 +135,8 @@
     reda = Reduce(sa, sa0, sa1, sa2, sema, (to_c, to_x, to_y), c, x, y)
     redb = Reduce(sb, sb0, sb1, sb2, semb, (to_c, to_y, to_x), c, y, x)
 
-    def forward(fresh):
+    def forward(lo, hi):
         def body(i, carry):
-            if fresh:
-                for cp in load(i):
-                    cp.wait()
             xc = xs[i]
             h = dot(xc, w1[i], 1, 0).astype(BF16).astype(F32)
             h2 = h * h
@@ -155,7 +148,7 @@
             xs[i + 1] = (xc.astype(F32) + dot(a, w2[i], 1, 0)).astype(BF16)
             return carry
 
-        lax.fori_loop(0, layers, body, 0)
+        lax.fori_loop(lo, hi, body, 0, unroll=3)
 
     def block_backward(i, first, final):
         gc = gs[i + 1]
@@ -213,24 +206,33 @@
     send_dx1 = remote(dxs.at[1], dxs.at[1], zsem.at[2], zsem.at[3], to_z)
     send_dx0 = remote(gs.at[0], dxs.at[0], zsem.at[4], zsem.at[5], to_z)
 
+    next_x = pltpu.make_async_copy(x_in.at[0, 0], dxs.at[0], asem.at[4])
+    for lo, hi in ((0, 3), (3, layers)):
+        for i in range(lo, hi):
+            for cp in load(i):
+                cp.wait()
+        forward(lo, hi)
+        if lo == 0:
+            load_g.start()
+            load_acc1.start()
+            load_acc2.start()
+            load_emb(lambda cp: cp.start())
+            pl.when(pp == 0)(next_x.start)
+    load_acc1.wait()
+    load_acc2.wait()
+    load_g.wait()
+    enter()
+
     @pl.when(pp == 1)
     def _():
-        forward(True)
-        load_acc1.wait()
-        load_acc2.wait()
-        load_g.wait()
-
         def step(k, carry):
             @pl.when(k == layers)
             def _():
                 send_cot.start()
 
-            when_layer(k, 1, start0)
-            when_layer(k, 3, start1)
-            when_layer(k, 6, start2)
-            when_layer(k, 0, lambda i: block_backward(i, True, True))
-            when_layer(k, 2, add0)
-            when_layer(k, 5, add1)
+            when_layer(k, 0, lambda i: (block_backward(i, True, True), start0(i)))
+            when_layer(k, 2, lambda i: (add0(i), start1(i)))
+            when_layer(k, 5, lambda i: (add1(i), start2(i)))
             when_layer(k, 8, finish)
             return carry
 
@@ -243,23 +245,16 @@
 
     @pl.when(pp == 0)
     def _():
-        next_x = pltpu.make_async_copy(x_in.at[0, 0], dxs.at[0], asem.at[4])
-        next_x.start()
-        forward(True)
-        load_acc1.wait()
-        load_acc2.wait()
-        load_g.wait()
-
         def back(k, carry):
             block_backward(layers - 1 - k, True, False)
             return carry
 
-        lax.fori_loop(0, layers, back, 0)
+        lax.fori_loop(0, layers, back, 0, unroll=3)
         dxs[1] = gs[0]
         send_dx1.start()
         next_x.wait()
         xs[0] = dxs[0]
-        forward(False)
+        forward(0, layers)
         dxt[:, pl.ds(tokens, tokens)] = dxs[1].T
         send_cot.wait_recv()
         gs[layers] = cot_in[...]
@@ -269,13 +264,11 @@
             def _():
                 send_dx0.start()
 
-            when_layer(k, 1, start0)
-            when_layer(k, 3, start1)
-            when_layer(k, 0, lambda i: block_backward(i, False, True))
-            when_layer(k, 2, add0)
+            when_layer(k, 0, lambda i: (block_backward(i, False, True), start0(i)))
+            when_layer(k, 2, lambda i: (add0(i), start1(i)))
             return carry
 
-        lax.fori_loop(0, layers + 4, step, 0)
+        lax.fori_loop(0, layers + 2, step, 0)
         dxt[:, pl.ds(0, tokens)] = gs[0].T
         send_dx1.wait_send()
         send_dx0.wait_send()
@@ -328,21 +321,16 @@
                 def _():
                     fn(layers - 1 - at)
 
-        late(1, start2)
-        stage(1, lambda i: (reda.copy0(i).start(), redb.copy0(i).start()))
-        stage(2, lambda i: (reda.copy1(i).start(), redb.copy1(i).start()))
-        stage(4, lambda i: (reda.copy2(i).start(), redb.copy2(i).start()))
-        stage(6, lambda i: [cp.start() for cp in zcopy(i)])
-        stage(0, build)
-        late(0, add1)
-        stage(1, lambda i: (reda.add0(i), redb.add0(i)))
-        stage(3, lambda i: (reda.add1(i), redb.add1(i)))
-        stage(5, emb_finish)
+        stage(0, lambda i: (build(i), reda.copy0(i).start(), redb.copy0(i).start()))
+        late(0, lambda i: (add1(i), start2(i)))
+        stage(1, lambda i: (reda.add0(i), redb.add0(i), reda.copy1(i).start(), redb.copy1(i).start()))
+        stage(3, lambda i: (reda.add1(i), redb.add1(i), reda.copy2(i).start(), redb.copy2(i).start()))
+        stage(5, lambda i: (emb_finish(i), [cp.start() for cp in zcopy(i)]))
         late(4, finish)
-        stage(8, put)
+        stage(7, put)
         return carry
 
-    lax.fori_loop(0, pairs + 9, emb_step, 0)
+    lax.fori_loop(0, pairs + 8, emb_step, 0)
 
     def drain_layer(i, carry):
         red1.drain(i)

time: 87.1 us -> 80.9 us (0.929)
  Pallas kernels: 86.3 us -> 80.1 us
    pallas_call x1, Pallas kernels: 83.3 us -> 77.1 us  [fused(): pl.pallas_call(functools.partial(fused_kernel, layers, pairs, width, voca...]
where the time goes in v4:
time: 80.9 us; the launch traced here: 80.8 us
  Pallas kernels  80.1 us (99%)
    pallas_call x1, Pallas kernels, fused(): pl.pallas_call(functools.partial(fused_kernel, layers, pairs, width, voca...  77.1 us
    pallas_call x1, Pallas kernels, mean(): pl.pallas_call(mean_kernel, out_shape=(jax.ShapeDtypeStruct(a.shape, F32)...  3.03 us

profile of v4, /device:TPU:0, one launch (start us, length us, event | category | flops | bytes accessed | tf_op | source)
XLA Modules:
  0.0 80.8 jit_solution(10744197309508258235)
XLA Ops:
  0.6 77.1 %shard_map.103 = (f32[12,16,512]{2,1,0:T(8,128)}, f32[12,64,128]{2,1,0:T(8,128)}, bf16[16,30720]{1,0:T(8,128)(2,1)}) custom-call(s32[2,512]{1,0:T(2,128)} %tok_ids.1, bf16[1,512,128]{2,1,0:T(8,128)(2,1)} %d_out.1, bf16[1,2,512,128]{3,2,1,0:T(8,128)(2,1)} %x_in.1, bf16[12,128,512]{2,1,0:T(8,128)(2,1)} %w_in.1, bf16[12,512,128]{2,1,0:T(8,128)(2,1)} %w_out.1, ...), custom_call_target="tpu_custom_call" | custom-call | tf_op jit(solution)/shard_map/pallas_call | solution.py:365
  77.7 3.0 %shard_map.104 = (f32[12,16,512]{2,1,0:T(8,128)}, f32[12,64,128]{2,1,0:T(8,128)}, f32[16,30522]{1,0:T(8,128)}) custom-call(f32[12,16,512]{2,1,0:T(8,128)} %get-tuple-element.9.a, f32[12,64,128]{2,1,0:T(8,128)} %get-tuple-element.10.b, bf16[16,30720]{1,0:T(8,128)(2,1)} %get-tuple-element.11.e), custom_call_target="tpu_custom_call" | custom-call | tf_op jit(solution)/shard_map/pallas_call | solution.py:413

commit v5 on v4

--- a/solution.py
+++ b/solution.py
@@ -89,7 +89,7 @@
 
 def fused_kernel(layers, pairs, width, vocab, tok_ids, d_out, x_in, w_in, w_out, acc_in, acc_out, acc_emb, g_in, g_out, emb_out,
                  w1, w2, xs, hid, slope, gs, dh, dw1, dw2, acc2, cot_in, dxs, s1, s1a, s1b, s1c, s2, s2a, s2b, s2c,
-                 rel, buf, dxt, sa, sa0, sa1, sa2, sb, sb0, sb1, sb2, fa, fb, za, zb,
+                 ids_in, rel, buf, dxt, sa, sa0, sa1, sa2, sb, sb0, sb1, sb2, fa, fb, za, zb,
                  wsem, asem, zsem, sem1, sem2, esem, sema, semb, fsem):
     pp, y, x, c, to_x, to_y, to_c, to_z = coords()
     tokens = dxs.shape[1]
@@ -117,17 +117,12 @@
     load_acc1 = pltpu.make_async_copy(acc_in.at[:, 0], dw1, asem.at[0])
     load_acc2 = pltpu.make_async_copy(acc_out.at[:, 0], acc2, asem.at[1])
     enter = knock((to_x, to_y, to_c, to_z))
+    load_ids = pltpu.make_async_copy(tok_ids, ids_in, asem.at[5])
     load_x.start()
     for i in range(layers):
         for cp in load(i):
             cp.start()
 
-    lane = lax.broadcasted_iota(jnp.int32, (128, 128), 1)
-    for j in range(2):
-        for b in range(tokens // 128):
-            ids = tok_ids[j:j + 1, b * 128:(b + 1) * 128].astype(F32)
-            ids = jnp.broadcast_to(ids, (128, 128)).T.astype(jnp.int32)
-            rel[pl.ds(j * tokens + b * 128, 128)] = ids - lane
     load_x.wait()
 
     red1 = Reduce(s1, s1a, s1b, s1c, sem1, (to_c, to_x, to_y), c, x, y)
@@ -197,10 +192,15 @@
         g_in[i] = red1.last(i)
         g_out[i] = red2.last(i)
 
-    def when_layer(k, lag, fn):
-        @pl.when((k >= lag) & (k < layers + lag))
+    group = 2
+    groups = layers // group
+
+    def when_group(k, lag, *fns):
+        @pl.when((k >= lag) & (k < groups + lag))
         def _():
-            fn(layers - 1 - (k - lag))
+            for fn in fns:
+                for n in range(group):
+                    fn(layers - 1 - (k - lag) * group - n)
 
     send_cot = remote(gs.at[0], cot_in, zsem.at[0], zsem.at[1], to_z)
     send_dx1 = remote(dxs.at[1], dxs.at[1], zsem.at[2], zsem.at[3], to_z)
@@ -216,28 +216,35 @@
             load_g.start()
             load_acc1.start()
             load_acc2.start()
+            load_ids.start()
             load_emb(lambda cp: cp.start())
             pl.when(pp == 0)(next_x.start)
     load_acc1.wait()
     load_acc2.wait()
     load_g.wait()
+    load_ids.wait()
+    lane = lax.broadcasted_iota(jnp.int32, (128, 128), 1)
+    for j in range(2):
+        for b in range(tokens // 128):
+            ids = ids_in[j:j + 1, b * 128:(b + 1) * 128].astype(F32)
+            ids = jnp.broadcast_to(ids, (128, 128)).T.astype(jnp.int32)
+            rel[pl.ds(j * tokens + b * 128, 128)] = ids - lane
     enter()
 
     @pl.when(pp == 1)
     def _():
         def step(k, carry):
-            @pl.when(k == layers)
+            @pl.when(k == groups)
             def _():
                 send_cot.start()
 
-            when_layer(k, 0, lambda i: (block_backward(i, True, True), start0(i)))
-            when_layer(k, 2, lambda i: (add0(i), start1(i)))
-            when_layer(k, 5, lambda i: (add1(i), start2(i)))
-            when_layer(k, 8, finish)
+            when_group(k, 0, lambda i: block_backward(i, True, True), start0)
+            when_group(k, 1, add0, start1)
+            when_group(k, 4, add1, start2)
+            when_group(k, 7, finish)
             return carry
 
-        lax.fori_loop(0, layers + 9, step, 0)
-        send_cot.wait_send()
+        lax.fori_loop(0, groups + 8, step, 0)
         send_dx1.wait_recv()
         dxt[:, pl.ds(tokens, tokens)] = dxs[1].T
         send_dx0.wait_recv()
@@ -260,18 +267,16 @@
         gs[layers] = cot_in[...]
 
         def step(k, carry):
-            @pl.when(k == layers)
+            @pl.when(k == groups)
             def _():
                 send_dx0.start()
 
-            when_layer(k, 0, lambda i: (block_backward(i, False, True), start0(i)))
-            when_layer(k, 2, lambda i: (add0(i), start1(i)))
+            when_group(k, 0, lambda i: block_backward(i, False, True), start0)
+            when_group(k, 1, add0, start1)
             return carry
 
-        lax.fori_loop(0, layers + 2, step, 0)
+        lax.fori_loop(0, groups + 1, step, 0)
         dxt[:, pl.ds(0, tokens)] = gs[0].T
-        send_dx1.wait_send()
-        send_dx0.wait_send()
 
     load_emb(lambda cp: cp.wait())
 
@@ -332,6 +337,15 @@
 
     lax.fori_loop(0, pairs + 8, emb_step, 0)
 
+    @pl.when(pp == 1)
+    def _():
+        send_cot.wait_send()
+
+    @pl.when(pp == 0)
+    def _():
+        send_dx1.wait_send()
+        send_dx0.wait_send()
+
     def drain_layer(i, carry):
         red1.drain(i)
         red2.drain(i)
@@ -364,9 +378,8 @@
     piece = pltpu.VMEM((pairs, n1, width), BF16)
     return pl.pallas_call(
         functools.partial(fused_kernel, layers, pairs, width, vocab),
-        out_shape=(jax.ShapeDtypeStruct((layers, n1, ff), F32), jax.ShapeDtypeStruct((layers, n2, hid), F32),
-                   jax.ShapeDtypeStruct((n1, 2 * half), BF16)),
-        in_specs=[VM, ANY, ANY, ANY, ANY, ANY, ANY, ANY],
+        out_shape=(pltpu.VMEM((layers, n1, ff), F32), pltpu.VMEM((layers, n2, hid), F32), pltpu.VMEM((n1, 2 * half), BF16)),
+        in_specs=[ANY, ANY, ANY, ANY, ANY, ANY, ANY, ANY],
         out_specs=(VM, VM, VM),
         scratch_shapes=[
             pltpu.VMEM((layers, hid, ff), BF16),
@@ -383,6 +396,7 @@
             pltpu.VMEM((2, tokens, hid), BF16),
             *side(layers, n1, ff),
             *side(layers, n2, hid),
+            pltpu.VMEM((2, tokens), jnp.int32),
             pltpu.VMEM((2 * tokens, 128), jnp.int32),
             pltpu.VMEM((half, hid), F32),
             pltpu.VMEM((hid, 2 * tokens), BF16),
@@ -390,7 +404,7 @@
             *side(pairs, n1, width),
             piece, piece, piece, piece,
             pltpu.SemaphoreType.DMA((2, layers)),
-            pltpu.SemaphoreType.DMA((5,)),
+            pltpu.SemaphoreType.DMA((6,)),
             pltpu.SemaphoreType.DMA((6,)),
             pltpu.SemaphoreType.DMA((6, layers)),
             pltpu.SemaphoreType.DMA((6, layers)),
@@ -399,7 +413,7 @@
             pltpu.SemaphoreType.DMA((6, pairs)),
             pltpu.SemaphoreType.DMA((4, pairs)),
         ],
-        compiler_params=pltpu.CompilerParams(collective_id=0, has_side_effects=True, vmem_limit_bytes=67043328),
+        compiler_params=pltpu.CompilerParams(collective_id=0, has_side_effects=True, vmem_limit_bytes=65 * 10**6),
     )(tok_ids, d_out, stored_x, w_in, w_out, acc_in, acc_out, acc_emb)
 
 
@@ -415,6 +429,7 @@
         out_shape=(jax.ShapeDtypeStruct(a.shape, F32), jax.ShapeDtypeStruct(b.shape, F32), jax.ShapeDtypeStruct((e.shape[0], vocab), F32)),
         in_specs=[VM, VM, VM],
         out_specs=(VM, VM, VM),
+        compiler_params=pltpu.CompilerParams(vmem_limit_bytes=8 * 2**20),
     )(a, b, e)
 
 

time: 80.9 us -> 75.9 us (0.938)
  Pallas kernels: 80.1 us -> 75.2 us
    pallas_call x1, Pallas kernels: 77.1 us -> 73.5 us  [fused(): pl.pallas_call(functools.partial(fused_kernel, layers, pairs, width, voca...]
    pallas_call x1, Pallas kernels: 3.03 us -> 1.64 us  [mean(): pl.pallas_call(mean_kernel, out_shape=(jax.ShapeDtypeStruct(a.shape, F32)...]
where the time goes in v5:
time: 75.9 us; the launch traced here: 75.8 us
  Pallas kernels  75.2 us (99%)
    pallas_call x1, Pallas kernels, fused(): pl.pallas_call(functools.partial(fused_kernel, layers, pairs, width, voca...  73.5 us
    pallas_call x1, Pallas kernels, mean(): pl.pallas_call(mean_kernel, out_shape=(jax.ShapeDtypeStruct(a.shape, F32)...  1.64 us

profile of v5, /device:TPU:0, one launch (start us, length us, event | category | flops | bytes accessed | tf_op | source)
XLA Modules:
  0.0 75.8 jit_solution(12764783012884559082)
XLA Ops:
  0.6 73.5 %shard_map.103 = (f32[12,16,512]{2,1,0:T(8,128)S(1)}, f32[12,64,128]{2,1,0:T(8,128)S(1)}, bf16[16,30720]{1,0:T(8,128)(2,1)S(1)}) custom-call(s32[2,512]{1,0:T(2,128)} %tok_ids.1, bf16[1,512,128]{2,1,0:T(8,128)(2,1)} %d_out.1, bf16[1,2,512,128]{3,2,1,0:T(8,128)(2,1)} %x_in.1, bf16[12,128,512]{2,1,0:T(8,128)(2,1)} %w_in.1, bf16[12,512,128]{2,1,0:T(8,128)(2,1)} %w_out.1, ...), custom_call_target="tpu_custom_call" | custom-call | tf_op jit(solution)/shard_map/pallas_call | solution.py:379
  74.2 1.6 %shard_map.104 = (f32[12,16,512]{2,1,0:T(8,128)}, f32[12,64,128]{2,1,0:T(8,128)}, f32[16,30522]{1,0:T(8,128)}) custom-call(f32[12,16,512]{2,1,0:T(8,128)S(1)} %get-tuple-element.9.a, f32[12,64,128]{2,1,0:T(8,128)S(1)} %get-tuple-element.10.b, bf16[16,30720]{1,0:T(8,128)(2,1)S(1)} %get-tuple-element.11.e), custom_call_target="tpu_custom_call" | custom-call | tf_op jit(solution)/shard_map/pallas_call | solution.py:427

commit v6 on v5

--- a/solution.py
+++ b/solution.py
@@ -143,14 +143,16 @@
             xs[i + 1] = (xc.astype(F32) + dot(a, w2[i], 1, 0)).astype(BF16)
             return carry
 
-        lax.fori_loop(lo, hi, body, 0, unroll=3)
-
-    def block_backward(i, first, final):
+        lax.fori_loop(lo, hi, body, 0, unroll=hi - lo)
+
+    def block_backward(i, first, final, then=None):
         gc = gs[i + 1]
         da = dot(gc, w2[i], 1, 1).astype(BF16).astype(F32)
         dhc = (da * slope[i]).astype(BF16)
         dh[...] = dhc
         gs[i] = (gc.astype(F32) + dot(dhc, w1[i], 1, 1)).astype(BF16)
+        if then is not None:
+            then()
         new2 = dot(gs[i + 1], hid[i], 0, 0)
         if not first:
             new2 = new2 + dw2[i]
@@ -192,15 +194,11 @@
         g_in[i] = red1.last(i)
         g_out[i] = red2.last(i)
 
-    group = 2
-    groups = layers // group
-
-    def when_group(k, lag, *fns):
-        @pl.when((k >= lag) & (k < groups + lag))
+    def when_layer(k, lag, *fns):
+        @pl.when((k >= lag) & (k < layers + lag))
         def _():
             for fn in fns:
-                for n in range(group):
-                    fn(layers - 1 - (k - lag) * group - n)
+                fn(layers - 1 - (k - lag))
 
     send_cot = remote(gs.at[0], cot_in, zsem.at[0], zsem.at[1], to_z)
     send_dx1 = remote(dxs.at[1], dxs.at[1], zsem.at[2], zsem.at[3], to_z)
@@ -233,18 +231,28 @@
 
     @pl.when(pp == 1)
     def _():
+        def last_block(k, carry):
+            block_backward(layers - 1 - k, True, True)
+            return carry
+
+        def send_block(k, carry):
+            start0(layers - 1 - k)
+            return carry
+
+        middle = layers // 2
+        lax.fori_loop(0, middle, last_block, 0, unroll=3)
+        lax.fori_loop(0, middle, send_block, 0)
+        lax.fori_loop(middle, layers, last_block, 0, unroll=3)
+        send_cot.start()
+        lax.fori_loop(middle, layers, send_block, 0)
+
         def step(k, carry):
-            @pl.when(k == groups)
-            def _():
-                send_cot.start()
-
-            when_group(k, 0, lambda i: block_backward(i, True, True), start0)
-            when_group(k, 1, add0, start1)
-            when_group(k, 4, add1, start2)
-            when_group(k, 7, finish)
+            when_layer(k, 0, add0, start1)
+            when_layer(k, 3, add1, start2)
+            when_layer(k, 6, finish)
             return carry
 
-        lax.fori_loop(0, groups + 8, step, 0)
+        lax.fori_loop(0, layers + 6, step, 0)
         send_dx1.wait_recv()
         dxt[:, pl.ds(tokens, tokens)] = dxs[1].T
         send_dx0.wait_recv()
@@ -256,7 +264,7 @@
             block_backward(layers - 1 - k, True, False)
             return carry
 
-        lax.fori_loop(0, layers, back, 0, unroll=3)
+        lax.fori_loop(0, layers, back, 0, unroll=layers)
         dxs[1] = gs[0]
         send_dx1.start()
         next_x.wait()
@@ -266,16 +274,15 @@
         send_cot.wait_recv()
         gs[layers] = cot_in[...]
 
-        def step(k, carry):
-            @pl.when(k == groups)
-            def _():
-                send_dx0.start()
-
-            when_group(k, 0, lambda i: block_backward(i, False, True), start0)
-            when_group(k, 1, add0, start1)
-            return carry
-
-        lax.fori_loop(0, groups + 1, step, 0)
+        for i in reversed(range(layers)):
+            block_backward(i, False, True, send_dx0.start if i == 0 else None)
+            start0(i)
+            if i + 2 < layers:
+                add0(i + 2)
+                start1(i + 2)
+        for i in (1, 0):
+            add0(i)
+            start1(i)
         dxt[:, pl.ds(0, tokens)] = gs[0].T
 
     load_emb(lambda cp: cp.wait())

time: 75.9 us -> 72.4 us (0.954)
  Pallas kernels: 75.2 us -> 71.6 us
    pallas_call x1, Pallas kernels: 73.5 us -> 70 us  [fused(): pl.pallas_call(functools.partial(fused_kernel, layers, pairs, width, voca...]
where the time goes in v6:
time: 72.4 us; the launch traced here: 72.3 us
  Pallas kernels  71.6 us (99%)
    pallas_call x1, Pallas kernels, fused(): pl.pallas_call(functools.partial(fused_kernel, layers, pairs, width, voca...  70 us
    pallas_call x1, Pallas kernels, mean(): pl.pallas_call(mean_kernel, out_shape=(jax.ShapeDtypeStruct(a.shape, F32)...  1.64 us

profile of v6, /device:TPU:0, one launch (start us, length us, event | category | flops | bytes accessed | tf_op | source)
XLA Modules:
  0.0 72.3 jit_solution(4060167747692063671)
XLA Ops:
  0.6 70.0 %shard_map.103 = (f32[12,16,512]{2,1,0:T(8,128)S(1)}, f32[12,64,128]{2,1,0:T(8,128)S(1)}, bf16[16,30720]{1,0:T(8,128)(2,1)S(1)}) custom-call(s32[2,512]{1,0:T(2,128)} %tok_ids.1, bf16[1,512,128]{2,1,0:T(8,128)(2,1)} %d_out.1, bf16[1,2,512,128]{3,2,1,0:T(8,128)(2,1)} %x_in.1, bf16[12,128,512]{2,1,0:T(8,128)(2,1)} %w_in.1, bf16[12,512,128]{2,1,0:T(8,128)(2,1)} %w_out.1, ...), custom_call_target="tpu_custom_call" | custom-call | tf_op jit(solution)/shard_map/pallas_call | solution.py:386
  70.6 1.6 %shard_map.104 = (f32[12,16,512]{2,1,0:T(8,128)}, f32[12,64,128]{2,1,0:T(8,128)}, f32[16,30522]{1,0:T(8,128)}) custom-call(f32[12,16,512]{2,1,0:T(8,128)S(1)} %get-tuple-element.9.a, f32[12,64,128]{2,1,0:T(8,128)S(1)} %get-tuple-element.10.b, bf16[16,30720]{1,0:T(8,128)(2,1)S(1)} %get-tuple-element.11.e), custom_call_target="tpu_custom_call" | custom-call | tf_op jit(solution)/shard_map/pallas_call | solution.py:434

commit v7 on v6

--- a/solution.py
+++ b/solution.py
@@ -87,13 +87,15 @@
     return lax.dot_general(a, b, (((ca,), (cb,)), ((), ())), preferred_element_type=F32)
 
 
-def fused_kernel(layers, pairs, width, vocab, tok_ids, d_out, x_in, w_in, w_out, acc_in, acc_out, acc_emb, g_in, g_out, emb_out,
+def fused_kernel(layers, pairs, split, width, vocab, tok_ids, d_out, x_in, w_in, w_out, acc_in, acc_out, acc_emb, g_in, g_out, emb_out,
                  w1, w2, xs, hid, slope, gs, dh, dw1, dw2, acc2, cot_in, dxs, s1, s1a, s1b, s1c, s2, s2a, s2b, s2c,
-                 ids_in, rel, buf, dxt, sa, sa0, sa1, sa2, sb, sb0, sb1, sb2, fa, fb, za, zb,
+                 ids_in, rel, buf, dxt, sa, sa0, sa1, sa2, sb, sb0, sb1, sb2, za, zb,
                  wsem, asem, zsem, sem1, sem2, esem, sema, semb, fsem):
     pp, y, x, c, to_x, to_y, to_c, to_z = coords()
     tokens = dxs.shape[1]
-    half = 2 * pairs * width
+    head = 2 * split * width
+    mine, theirs = split + pp * (pairs - split), pairs - pp * (pairs - split)
+    my_row, their_row = pp * head, (1 - pp) * head
     block = width
 
     def load(i):
@@ -106,14 +108,14 @@
 
         @pl.when(pp == 0)
         def _():
-            one(half, 0)
+            one(head, 0)
 
         @pl.when(pp == 1)
         def _():
-            one(vocab - half, half)
+            one(vocab - head, head)
 
     load_x = pltpu.make_async_copy(x_in.at[0, 1 - pp], xs.at[0], asem.at[2])
-    load_g = pltpu.make_async_copy(d_out.at[0], gs.at[layers], asem.at[3])
+    load_g = pltpu.make_async_copy(d_out.at[0], gs.at[layers % 2], asem.at[3])
     load_acc1 = pltpu.make_async_copy(acc_in.at[:, 0], dw1, asem.at[0])
     load_acc2 = pltpu.make_async_copy(acc_out.at[:, 0], acc2, asem.at[1])
     enter = knock((to_x, to_y, to_c, to_z))
@@ -146,14 +148,14 @@
         lax.fori_loop(lo, hi, body, 0, unroll=hi - lo)
 
     def block_backward(i, first, final, then=None):
-        gc = gs[i + 1]
+        gc = gs[(i + 1) % 2]
         da = dot(gc, w2[i], 1, 1).astype(BF16).astype(F32)
         dhc = (da * slope[i]).astype(BF16)
         dh[...] = dhc
-        gs[i] = (gc.astype(F32) + dot(dhc, w1[i], 1, 1)).astype(BF16)
+        gs[i % 2] = (gc.astype(F32) + dot(dhc, w1[i], 1, 1)).astype(BF16)
         if then is not None:
             then()
-        new2 = dot(gs[i + 1], hid[i], 0, 0)
+        new2 = dot(gs[(i + 1) % 2], hid[i], 0, 0)
         if not first:
             new2 = new2 + dw2[i]
         new1 = dot(xs[i], dh[...], 0, 0) + dw1[i]
@@ -231,28 +233,34 @@
 
     @pl.when(pp == 1)
     def _():
-        def last_block(k, carry):
-            block_backward(layers - 1 - k, True, True)
+        group = 3
+
+        def blocks(k, carry):
+            for n in range(group):
+                block_backward(layers - 1 - k * group - n, True, True)
+            for n in range(group):
+                start0(layers - 1 - k * group - n)
+
+            @pl.when(k >= 1)
+            def _():
+                for n in range(group):
+                    add0(layers - 1 - (k - 1) * group - n)
+                    start1(layers - 1 - (k - 1) * group - n)
+
             return carry
 
-        def send_block(k, carry):
-            start0(layers - 1 - k)
+        lax.fori_loop(0, layers // group, blocks, 0)
+        send_cot.start()
+        for i in reversed(range(group)):
+            add0(i)
+            start1(i)
+
+        def step(k, carry):
+            when_layer(k, 0, add1, start2)
+            when_layer(k, 3, finish)
             return carry
 
-        middle = layers // 2
-        lax.fori_loop(0, middle, last_block, 0, unroll=3)
-        lax.fori_loop(0, middle, send_block, 0)
-        lax.fori_loop(middle, layers, last_block, 0, unroll=3)
-        send_cot.start()
-        lax.fori_loop(middle, layers, send_block, 0)
-
-        def step(k, carry):
-            when_layer(k, 0, add0, start1)
-            when_layer(k, 3, add1, start2)
-            when_layer(k, 6, finish)
-            return carry
-
-        lax.fori_loop(0, layers + 6, step, 0)
+        lax.fori_loop(0, layers + 3, step, 0)
         send_dx1.wait_recv()
         dxt[:, pl.ds(tokens, tokens)] = dxs[1].T
         send_dx0.wait_recv()
@@ -272,7 +280,7 @@
         forward(0, layers)
         dxt[:, pl.ds(tokens, tokens)] = dxs[1].T
         send_cot.wait_recv()
-        gs[layers] = cot_in[...]
+        gs[layers % 2] = cot_in[...]
 
         for i in reversed(range(layers)):
             block_backward(i, False, True, send_dx0.start if i == 0 else None)
@@ -287,16 +295,19 @@
 
     load_emb(lambda cp: cp.wait())
 
+    def own(red):
+        return 4 * red.c + 2 * red.p + red.q
+
     def zcopy(i):
-        return (remote(fa.at[i], za.at[i], fsem.at[0, i], fsem.at[1, i], to_z),
-                remote(fb.at[i], zb.at[i], fsem.at[2, i], fsem.at[3, i], to_z))
+        return (remote(sa.at[i, own(reda)], za.at[i], fsem.at[0, i], fsem.at[1, i], to_z),
+                remote(sb.at[i, own(redb)], zb.at[i], fsem.at[2, i], fsem.at[3, i], to_z))
 
     def build(i):
         for part, dst, slab in ((0, sa, slab_xy), (1, sb, slab_yx)):
             def piece(j, carry):
                 at = pl.multiple_of(j * block, block)
                 row = pl.multiple_of((2 * i + part) * width + j * block, block)
-                base = pp * half + row
+                base = my_row + row
                 ids = rel[...]
                 hot = jnp.concatenate([jnp.where(ids == base + 128 * n, 1.0, 0.0).astype(BF16) for n in range(block // 128)], axis=1)
                 val = buf[pl.ds(row, block), :].T + dot(dxt[...], hot, 1, 0)
@@ -307,21 +318,26 @@
 
             lax.fori_loop(0, width // block, piece, 0)
 
+    def lanes(row, i, part):
+        return pl.ds(pl.multiple_of(row + (2 * i + part) * width, 128), width)
+
     def emb_finish(i):
-        fa[i] = reda.last(i).astype(BF16)
-        fb[i] = redb.last(i).astype(BF16)
+        for part, red in ((0, reda), (1, redb)):
+            val = red.last(i).astype(BF16)
+            red.src[i, own(red)] = val
+            emb_out[:, lanes(my_row, i, part)] = val
+        for cp in zcopy(i):
+            cp.start()
 
     def put(i):
         for cp in zcopy(i):
             cp.wait_recv()
-        for part, mine, other in ((0, fa, za), (1, fb, zb)):
-            off = (2 * i + part) * width
-            emb_out[:, pl.ds(pl.multiple_of(pp * half + off, 128), width)] = mine[i]
-            emb_out[:, pl.ds(pl.multiple_of((1 - pp) * half + off, 128), width)] = other[i]
+        emb_out[:, lanes(their_row, i, 0)] = za[i]
+        emb_out[:, lanes(their_row, i, 1)] = zb[i]
 
     def emb_step(k, carry):
-        def stage(lag, fn):
-            @pl.when((k >= lag) & (k < pairs + lag))
+        def stage(lag, fn, count=mine):
+            @pl.when((k >= lag) & (k < count + lag))
             def _():
                 fn(k - lag)
 
@@ -337,9 +353,9 @@
         late(0, lambda i: (add1(i), start2(i)))
         stage(1, lambda i: (reda.add0(i), redb.add0(i), reda.copy1(i).start(), redb.copy1(i).start()))
         stage(3, lambda i: (reda.add1(i), redb.add1(i), reda.copy2(i).start(), redb.copy2(i).start()))
-        stage(5, lambda i: (emb_finish(i), [cp.start() for cp in zcopy(i)]))
+        stage(5, emb_finish)
         late(4, finish)
-        stage(7, put)
+        stage(7, put, theirs)
         return carry
 
     lax.fori_loop(0, pairs + 8, emb_step, 0)
@@ -361,10 +377,13 @@
     lax.fori_loop(0, layers, drain_layer, 0)
 
     def drain_pair(i, carry):
-        reda.drain(i)
-        redb.drain(i)
-        for cp in zcopy(i):
-            cp.wait_send()
+        @pl.when(i < mine)
+        def _():
+            reda.drain(i)
+            redb.drain(i)
+            for cp in zcopy(i):
+                cp.wait_send()
+
         return carry
 
     lax.fori_loop(0, pairs, drain_pair, 0)
@@ -374,7 +393,8 @@
     layers, hid, ff = w_in.shape
     tokens = d_out.shape[1]
     vocab = acc_emb.shape[0]
-    pairs, width = 10, 768
+    split, width = 9, 768
+    pairs = pl.cdiv(vocab, 2 * width) - split
     half = 2 * pairs * width
     n1, n2 = hid // 8, ff // 8
 
@@ -384,8 +404,8 @@
 
     piece = pltpu.VMEM((pairs, n1, width), BF16)
     return pl.pallas_call(
-        functools.partial(fused_kernel, layers, pairs, width, vocab),
-        out_shape=(pltpu.VMEM((layers, n1, ff), F32), pltpu.VMEM((layers, n2, hid), F32), pltpu.VMEM((n1, 2 * half), BF16)),
+        functools.partial(fused_kernel, layers, pairs, split, width, vocab),
+        out_shape=(pltpu.VMEM((layers, n1, ff), F32), pltpu.VMEM((layers, n2, hid), F32), pltpu.VMEM((n1, 2 * (pairs + split) * width), BF16)),
         in_specs=[ANY, ANY, ANY, ANY, ANY, ANY, ANY, ANY],
         out_specs=(VM, VM, VM),
         scratch_shapes=[
@@ -394,7 +414,7 @@
             pltpu.VMEM((layers + 1, tokens, hid), BF16),
             pltpu.VMEM((layers, tokens, ff), BF16),
             pltpu.VMEM((layers, tokens, ff), F32),
-            pltpu.VMEM((layers + 1, tokens, hid), BF16),
+            pltpu.VMEM((2, tokens, hid), BF16),
             pltpu.VMEM((tokens, ff), BF16),
             pltpu.VMEM((layers, hid, ff), F32),
             pltpu.VMEM((layers, hid, ff), F32),
@@ -409,7 +429,7 @@
             pltpu.VMEM((hid, 2 * tokens), BF16),
             *side(pairs, n1, width),
             *side(pairs, n1, width),
-            piece, piece, piece, piece,
+            piece, piece,
             pltpu.SemaphoreType.DMA((2, layers)),
             pltpu.SemaphoreType.DMA((6,)),
             pltpu.SemaphoreType.DMA((6,)),

time: 72.4 us -> 73.8 us (1.019)
  Pallas kernels: 71.6 us -> 73 us
    pallas_call x1, Pallas kernels: 70 us -> 71.4 us  [fused(): pl.pallas_call(functools.partial(fused_kernel, layers, pairs, split, widt...]
where the time goes in v7:
time: 73.8 us; the launch traced here: 73.7 us
  Pallas kernels  73 us (99%)
    pallas_call x1, Pallas kernels, fused(): pl.pallas_call(functools.partial(fused_kernel, layers, pairs, split, widt...  71.4 us
    pallas_call x1, Pallas kernels, mean(): pl.pallas_call(mean_kernel, out_shape=(jax.ShapeDtypeStruct(a.shape, F32)...  1.64 us

profile of v7, /device:TPU:0, one launch (start us, length us, event | category | flops | bytes accessed | tf_op | source)
XLA Modules:
  0.0 73.7 jit_solution(2819822481525147537)
XLA Ops:
  0.6 71.4 %shard_map.103 = (f32[12,16,512]{2,1,0:T(8,128)S(1)}, f32[12,64,128]{2,1,0:T(8,128)S(1)}, bf16[16,30720]{1,0:T(8,128)(2,1)S(1)}) custom-call(s32[2,512]{1,0:T(2,128)} %tok_ids.1, bf16[1,512,128]{2,1,0:T(8,128)(2,1)} %d_out.1, bf16[1,2,512,128]{3,2,1,0:T(8,128)(2,1)} %x_in.1, bf16[12,128,512]{2,1,0:T(8,128)(2,1)} %w_in.1, bf16[12,512,128]{2,1,0:T(8,128)(2,1)} %w_out.1, ...), custom_call_target="tpu_custom_call" | custom-call | tf_op jit(solution)/shard_map/pallas_call | solution.py:406
  72.0 1.6 %shard_map.104 = (f32[12,16,512]{2,1,0:T(8,128)}, f32[12,64,128]{2,1,0:T(8,128)}, f32[16,30522]{1,0:T(8,128)}) custom-call(f32[12,16,512]{2,1,0:T(8,128)S(1)} %get-tuple-element.9.a, f32[12,64,128]{2,1,0:T(8,128)S(1)} %get-tuple-element.10.b, bf16[16,30720]{1,0:T(8,128)(2,1)S(1)} %get-tuple-element.11.e), custom_call_target="tpu_custom_call" | custom-call | tf_op jit(solution)/shard_map/pallas_call | solution.py:454

commit v8 on v7

--- a/solution.py
+++ b/solution.py
@@ -358,7 +358,7 @@
         stage(7, put, theirs)
         return carry
 
-    lax.fori_loop(0, pairs + 8, emb_step, 0)
+    lax.fori_loop(0, max(pairs, split) + 8, emb_step, 0)
 
     @pl.when(pp == 1)
     def _():
@@ -386,23 +386,23 @@
 
         return carry
 
-    lax.fori_loop(0, pairs, drain_pair, 0)
+    lax.fori_loop(0, max(pairs, split), drain_pair, 0)
 
 
 def fused(tok_ids, d_out, stored_x, w_in, w_out, acc_in, acc_out, acc_emb):
     layers, hid, ff = w_in.shape
     tokens = d_out.shape[1]
     vocab = acc_emb.shape[0]
-    split, width = 9, 768
+    split, width = 11, 768
     pairs = pl.cdiv(vocab, 2 * width) - split
-    half = 2 * pairs * width
+    most = max(pairs, split)
     n1, n2 = hid // 8, ff // 8
 
     def side(count, *shape):
         return [pltpu.VMEM((count, 8, *shape), BF16), pltpu.VMEM((count, 4, *shape), BF16),
                 pltpu.VMEM((count, 2, *shape), BF16), pltpu.VMEM((count, *shape), BF16)]
 
-    piece = pltpu.VMEM((pairs, n1, width), BF16)
+    piece = pltpu.VMEM((most, n1, width), BF16)
     return pl.pallas_call(
         functools.partial(fused_kernel, layers, pairs, split, width, vocab),
         out_shape=(pltpu.VMEM((layers, n1, ff), F32), pltpu.VMEM((layers, n2, hid), F32), pltpu.VMEM((n1, 2 * (pairs + split) * width), BF16)),
@@ -425,10 +425,10 @@
             *side(layers, n2, hid),
             pltpu.VMEM((2, tokens), jnp.int32),
             pltpu.VMEM((2 * tokens, 128), jnp.int32),
-            pltpu.VMEM((half, hid), F32),
+            pltpu.VMEM((2 * most * width, hid), F32),
             pltpu.VMEM((hid, 2 * tokens), BF16),
-            *side(pairs, n1, width),
-            *side(pairs, n1, width),
+            *side(most, n1, width),
+            *side(most, n1, width),
             piece, piece,
             pltpu.SemaphoreType.DMA((2, layers)),
             pltpu.SemaphoreType.DMA((6,)),
@@ -436,9 +436,9 @@
             pltpu.SemaphoreType.DMA((6, layers)),
             pltpu.SemaphoreType.DMA((6, layers)),
             pltpu.SemaphoreType.DMA,
-            pltpu.SemaphoreType.DMA((6, pairs)),
-            pltpu.SemaphoreType.DMA((6, pairs)),
-            pltpu.SemaphoreType.DMA((4, pairs)),
+            pltpu.SemaphoreType.DMA((6, most)),
+            pltpu.SemaphoreType.DMA((6, most)),
+            pltpu.SemaphoreType.DMA((4, most)),
         ],
         compiler_params=pltpu.CompilerParams(collective_id=0, has_side_effects=True, vmem_limit_bytes=65 * 10**6),
     )(tok_ids, d_out, stored_x, w_in, w_out, acc_in, acc_out, acc_emb)

time: 73.8 us -> 72.3 us (0.980)
  Pallas kernels: 73 us -> 71.5 us
    pallas_call x1, Pallas kernels: 71.4 us -> 69.9 us  [fused(): pl.pallas_call(functools.partial(fused_kernel, layers, pairs, split, widt...]
where the time goes in v8:
time: 72.3 us; the launch traced here: 72.2 us
  Pallas kernels  71.5 us (99%)
    pallas_call x1, Pallas kernels, fused(): pl.pallas_call(functools.partial(fused_kernel, layers, pairs, split, widt...  69.9 us
    pallas_call x1, Pallas kernels, mean(): pl.pallas_call(mean_kernel, out_shape=(jax.ShapeDtypeStruct(a.shape, F32)...  1.64 us

profile of v8, /device:TPU:0, one launch (start us, length us, event | category | flops | bytes accessed | tf_op | source)
XLA Modules:
  0.0 72.2 jit_solution(4089986085985360700)
XLA Ops:
  0.6 69.9 %shard_map.103 = (f32[12,16,512]{2,1,0:T(8,128)S(1)}, f32[12,64,128]{2,1,0:T(8,128)S(1)}, bf16[16,30720]{1,0:T(8,128)(2,1)S(1)}) custom-call(s32[2,512]{1,0:T(2,128)} %tok_ids.1, bf16[1,512,128]{2,1,0:T(8,128)(2,1)} %d_out.1, bf16[1,2,512,128]{3,2,1,0:T(8,128)(2,1)} %x_in.1, bf16[12,128,512]{2,1,0:T(8,128)(2,1)} %w_in.1, bf16[12,512,128]{2,1,0:T(8,128)(2,1)} %w_out.1, ...), custom_call_target="tpu_custom_call" | custom-call | tf_op jit(solution)/shard_map/pallas_call | solution.py:406
  70.5 1.6 %shard_map.104 = (f32[12,16,512]{2,1,0:T(8,128)}, f32[12,64,128]{2,1,0:T(8,128)}, f32[16,30522]{1,0:T(8,128)}) custom-call(f32[12,16,512]{2,1,0:T(8,128)S(1)} %get-tuple-element.9.a, f32[12,64,128]{2,1,0:T(8,128)S(1)} %get-tuple-element.10.b, bf16[16,30720]{1,0:T(8,128)(2,1)S(1)} %get-tuple-element.11.e), custom_call_target="tpu_custom_call" | custom-call | tf_op jit(solution)/shard_map/pallas_call | solution.py:454
